TPU v7x, 256 devices: a whole 4x4x8 slice. The times are simulated.
256 devices in a mesh: section: 8 (over x, core), dp: 32 (over y, z).
Axes of the slice: x: 4, y: 4, z: 8, core: 2. Of those that a mesh axis runs over, the one named last changes fastest.
Arguments:
- item_owner: int32 [8, 32, 128, 1], P('section', 'dp'), may hold values from 0 to 31; in each aligned block of 128 rows (0 to 127, 128 to 255, ..., all dimensions but the last counted through in order) at most 8 rows name the same one
- item_row: int32 [8, 32, 128], P('section', 'dp'), may hold values from 0 to 255
- lengths: int32 [8, 32], P(None, 'dp'), may hold values from 1 to 128
- table: bfloat16 [8192, 1024], P('dp'), may hold values from -6 to 6
- w_in: bfloat16 [8, 1024, 4096], P('section', 'dp'), may hold values from -0.1875 to 0.1875
- w_out: bfloat16 [8, 1024, 1024], P('section', 'dp'), may hold values from -0.1875 to 0.1875
- gain_in: float32 [8, 1024], P('section'), may hold values from 0.5 to 1.5
- gain_mid: float32 [8, 1024], P('section'), may hold values from 0.5 to 1.5
Outputs:
- states: bfloat16 [8, 32, 8, 128, 1024], P('section', 'dp')
Inputs may be any that keep to these rules, and one draw needn't show every extreme that they name: Among the 128 events of one history no value of item_owner appears more than 8 times; some history reaches 8.
All inputs are finite; a program needn't handle non-finite values.
Results may differ from a plain program's by a relative error of at most 0.029.
Values may be sent and summed in bfloat16 or wider, within the bound.
No kernel may reach another device: no remote copies, remote signals or barrier semaphores. Data moves between devices by JAX's collectives and lax.ppermute only.
A program may use at most 64 MiB of HBM per device.

v0:
```python
import jax
import jax.numpy as jnp
from jax import lax
from jax.sharding import Mesh
from jax.sharding import PartitionSpec as P

HEADS = 8
DP = ("dp_0", "dp_1")


EPS = 1e-05


def cut_along(shard, dim, count):
    lengths = shard.shape
    tiles = shard.reshape(*lengths[:dim], count, lengths[dim] // count, *lengths[dim + 1 :])
    return jnp.moveaxis(tiles, dim, 0)


def laid_out(tiles, dim):
    lengths = list(tiles.shape[1:])
    lengths[dim] *= tiles.shape[0]
    return jnp.moveaxis(tiles, 0, dim).reshape(lengths)


def moved_by_axis(tiles, axes, sequence):
    inside = tiles.shape[1:]
    out = tiles.reshape(*(lax.axis_size(a) for a in axes), *inside)
    for k in sequence:
        out = lax.all_to_all(out, axes[k], k, k, tiled=True)
    return out.reshape(-1, *inside)


def exchange_by_axis(shard, axes, sequence, split_dim, concat_dim):
    tiles = cut_along(shard, split_dim, lax.axis_size(axes))
    return laid_out(moved_by_axis(tiles, axes, sequence), concat_dim)


def side_by_side(arrays, axis, dim, along):
    ends, at = ([], 0)
    for a in arrays[:-1]:
        at += a.shape[along]
        ends.append(at)
    both = jnp.concatenate(arrays, axis=along)
    return tuple(jnp.split(lax.all_gather(both, axis, axis=dim, tiled=True), ends, axis=along))


def copy_for_each(shard, axis):
    copies = jnp.broadcast_to(shard, (lax.axis_size(axis), *shard.shape))
    return lax.all_to_all(copies, axis, split_axis=0, concat_axis=0, tiled=True)


def collect(shard, axis, dim):
    tiles = copy_for_each(shard, axis)
    return laid_out(tiles, dim)


def from_behind(block, axis, distance):
    devices = range(lax.axis_size(axis))
    route = [(i - distance, i) for i in devices if i - distance in devices]
    return lax.ppermute(block, axis, route)


def normalize(values):
    center = values - jnp.mean(values, axis=-1, keepdims=True)
    spread = jnp.mean(center * center, axis=-1, keepdims=True)
    return center * lax.rsqrt(spread + EPS)


def layer_part(current, length, weight_in, weight_out, scale_in, scale_mid):
    wide = current.astype(jnp.float32)
    normed = (normalize(wide) * scale_in).astype(jnp.bfloat16)
    uvqk = jax.nn.silu(jnp.dot(normed, weight_in, preferred_element_type=jnp.float32)).astype(
        jnp.bfloat16
    )
    u_part, v_part, q_part, k_part = jnp.split(uvqk, 4, axis=-1)
    rows = current.shape[0]
    head_width = current.shape[1] // HEADS
    position = jnp.arange(rows, dtype=jnp.int32)
    key_all, value_all = (k_part, v_part)
    key_ok = position >= 0
    count = key_all.shape[0]
    queries = q_part.reshape(rows, HEADS, head_width)
    keys = key_all.reshape(count, HEADS, head_width)
    values = value_all.reshape(count, HEADS, head_width)
    scores = jnp.einsum("qhd,khd->hqk", queries, keys, preferred_element_type=jnp.float32)
    allowed = (
        (position[None, :] <= position[:, None]) & (position[None, :] < length) & key_ok[None, :]
    )
    weights = jnp.where(
        allowed[None], jax.nn.silu(scores / jnp.sqrt(jnp.float32(head_width))), 0.0
    ).astype(jnp.bfloat16)
    attn = jnp.einsum("hqk,khd->qhd", weights, values, preferred_element_type=jnp.float32).reshape(
        rows, HEADS * head_width
    )
    mixed = (normalize(attn) * scale_mid * u_part.astype(jnp.float32)).astype(jnp.bfloat16)
    result = (jnp.dot(mixed, weight_out, preferred_element_type=jnp.float32) + wide).astype(
        jnp.bfloat16
    )
    return (result, k_part, v_part)


def lookup_items(item_owner, item_row, table):
    groups = lax.axis_size(DP)
    owner = item_owner.reshape(-1)
    rows = item_row.reshape(-1)
    seq_len = rows.shape[0]
    slots_each = max(2, 2 * seq_len // groups)
    match = (owner[:, None] == jnp.arange(groups, dtype=jnp.int32)[None, :]).astype(jnp.int32)
    earlier = jnp.cumsum(match, axis=0) - match
    slot = jnp.sum(earlier * match, axis=1)
    placed = match[:, :, None] * (
        slot[:, None, None] == jnp.arange(slots_each, dtype=jnp.int32)[None, None, :]
    ).astype(jnp.int32)
    request = jnp.sum(placed * (rows + 1)[:, None, None], axis=0) - 1
    received = exchange_by_axis(request, DP, (0, 1), 0, 0)
    found = jnp.take(table, jnp.maximum(received, 0), axis=0)
    found = jnp.where((received >= 0)[:, :, None], found, jnp.zeros_like(found))
    answered = lax.all_to_all(found, DP, split_axis=0, concat_axis=0, tiled=True)
    flat_rows = answered.reshape(groups * slots_each, table.shape[1])
    return jnp.take(flat_rows, owner * slots_each + slot, axis=0)


def on_device(item_owner, item_row, lengths, table, w_in, w_out, gain_in, gain_mid):
    sections = lax.axis_size("section")
    here = lax.axis_index("section")
    micro = lengths.shape[0]
    lens = lengths[:, 0]
    embedded = lookup_items(item_owner, item_row, table)
    full_in, full_out = side_by_side((w_in, w_out), DP, 1, 2)
    weight_in = full_in[0]
    weight_out = full_out[0]
    scale_in = gain_in[0]
    scale_mid = gain_mid[0]
    seq_len = embedded.shape[0]
    inputs = collect(embedded[None], "section", 0)
    pieces = 1
    part_rows = seq_len // pieces
    ticks = pieces * micro + sections - 1
    blank = jnp.zeros((part_rows, embedded.shape[1]), jnp.bfloat16)

    def tick(step, carry):
        queue, incoming, kept_k, kept_v, saved = carry
        which = step - here
        valid = (which >= 0) & (which < pieces * micro)
        item = jnp.clip(which, 0, pieces * micro - 1)
        slot = item // pieces
        part = item % pieces
        offset = part * part_rows
        source = lax.dynamic_index_in_dim(
            inputs, jnp.clip(step // pieces, 0, micro - 1), 0, keepdims=False
        )
        current = jnp.where(here == 0, source, incoming)
        length = lax.dynamic_index_in_dim(lens, slot, 0, keepdims=False)

        def work(block):
            return layer_part(block, length, weight_in, weight_out, scale_in, scale_mid)

        def skip(block):
            return (block, blank, blank)

        finished, new_k, new_v = lax.cond(valid, work, skip, current)
        first = valid & (part == 0)
        kept_k = jnp.where(first, new_k, kept_k)
        kept_v = jnp.where(first, new_v, kept_v)
        previous = lax.dynamic_slice(saved, (slot, offset, 0), (1, part_rows, embedded.shape[1]))
        saved = lax.dynamic_update_slice(
            saved, jnp.where(valid, finished[None], previous), (slot, offset, 0)
        )
        incoming = from_behind(finished, "section", 1)
        return (queue, incoming, kept_k, kept_v, saved)

    start = (embedded, blank, blank, blank, jnp.zeros((micro,) + embedded.shape, jnp.bfloat16))
    queue, incoming, kept_k, kept_v, saved = lax.fori_loop(0, ticks, tick, start)
    return saved[None, None]


def solution(mesh):
    split = Mesh(mesh.devices.reshape(mesh.shape["section"], 4, 8), ("section", "dp_0", "dp_1"))
    placed = (
        P("section", DP, None, None),
        P("section", DP, None),
        P(None, DP),
        P(DP, None),
        P("section", DP, None),
        P("section", DP, None),
        P("section", None),
        P("section", None),
    )
    return jax.shard_map(
        on_device,
        mesh=split,
        in_specs=placed,
        out_specs=P("section", DP, None, None, None),
        check_vma=False,
    )
```

profile of v0, /device:TPU:6, one launch (start us, length us, event | category | flops | bytes accessed | tf_op | source)
XLA Modules:
  0.0 464.0 jit_solution(4642200611884954525)
XLA Ops:
  6.5 1.8 pad_maximum_fusion
  11.5 9.6 %all_to_all.20 = s32[4,8,1,8]{3,1,2,0:T(8,128)S(1)} all-to-all(s32[4,8,1,8]{3,1,2,0:T(8,128)S(1)} %add_bitcast_fusion), channel_id=1, replica_groups=mesh['section'=8,'dp_0'=4,'dp_1'=8] {'dp_0'}, dimensions={0} | all-to-all | bytes 2048 | tf_op jit(solution)/shard_map/all_to_all | solution.py:30
  21.1 16.1 %all_to_all.21 = s32[4,8,1,8]{3,0,2,1:T(4,128)S(1)} all-to-all(s32[4,8,1,8]{3,0,2,1:T(4,128)S(1)} %copy.46), channel_id=1, replica_groups=mesh['section'=8,'dp_0'=4,'dp_1'=8] {'dp_1'}, dimensions={1} | all-to-all | bytes 2048 | tf_op jit(solution)/shard_map/all_to_all | solution.py:30
  39.5 3.9 all-to-all-start.2
  43.5 17.8 %all-to-all-done.2 = bf16[32,8,1024]{2,1,0:T(8,128)(2,1)S(1)} async-done(((bf16[32,8,1024]{2,1,0:T(8,128)(2,1)}), bf16[32,8,1024]{2,1,0:T(8,128)(2,1)S(1)}, u32[]{:S(2)}, u32[]{:S(2)}) %all-to-all-start.2) | async-done | bytes 524320 | tf_op jit(solution)/shard_map/all_to_all | solution.py:119
  63.8 4.8 %all-to-all-start.3 = ((bf16[8,1,128,1024]{3,2,1,0:T(8,128)(2,1)}), bf16[8,1,128,1024]{3,2,1,0:T(8,128)(2,1)}, u32[]{:S(2)}, u32[]{:S(2)}) async-start(bf16[8,1,128,1024]{3,2,1,0:T(8,128)(2,1)} %broadcast_in_dim.94), calls=%async_computation.3 | async-start | bytes 4194304 | tf_op jit(solution)/shard_map/all_to_all | solution.py:50
  68.6 57.2 %all-gather.2.cloned.1.call-done = bf16[1,1024,5120]{2,1,0:T(8,128)(2,1)} async-done(((bf16[1,32,5120]{2,1,0:T(8,128)(2,1)}), bf16[1,1024,5120]{2,1,0:T(8,128)(2,1)}) %all-gather.2.cloned.1.call-update) | async-done | bytes 10485776 | tf_op jit(solution)/shard_map/all_gather | solution.py:45
  125.8 1.8 slice_bitcast_fusion.3
  127.6 7.8 %slice_bitcast_fusion.2 = bf16[1024,4096]{1,0:T(8,128)(2,1)} fusion(bf16[1,1024,5120]{2,1,0:T(8,128)(2,1)} %all-gather.2.cloned.1.call-done), kind=kLoop, calls=%fused_computation.50 | loop fusion | bytes 16777216 | tf_op jit(solution)/shard_map/squeeze | solution.py:131
  137.1 320.0 %while.18 = (s32[]{:T(128)}, bf16[128,1024]{1,0:T(8,128)(2,1)S(1)}, bf16[8,128,1024]{2,1,0:T(8,128)(2,1)}, s32[]{:T(128)}, pred[]{:T(512)}, /*index=5*/bf16[8,12...) while((s32[]{:T(128)}, bf16[128,1024]{1,0:T(8,128)(2,1)S(1)}, ...), condition=%wide.region_10.11_spmd, body=%wide.region_3.10_spmd.sunk | while | flops 1416266112 | bytes 27576472 | solution.py:174
  138.1 1.9 collective-permute-start
  140.0 1.7 fusion.50
  141.8 4.0 collective-permute-done
  146.8 1.9 collective-permute-start
  148.7 1.7 fusion.50
  150.5 4.0 collective-permute-done
  155.5 1.9 collective-permute-start
  157.4 1.7 fusion.50
  159.1 4.0 collective-permute-done
  164.2 1.9 collective-permute-start
  166.1 1.7 fusion.50
  167.8 4.0 collective-permute-done
  172.9 1.9 collective-permute-start
  174.8 1.7 fusion.50
  176.5 4.0 collective-permute-done
  181.6 1.9 collective-permute-start
  183.5 1.7 fusion.50
  185.2 72.5 %collective-permute-done = bf16[128,1024]{1,0:T(8,128)(2,1)S(1)} collective-permute-done((bf16[128,1024]{1,0:T(8,128)(2,1)S(1)}, bf16[128,1024]{1,0:T(8,128)(2,1)S(1)}, u32[]{:S(2)}, u32[]{:S(2)}) %collective-permute-start) | collective-permute-done | bytes 262176 | tf_op jit(solution)/shard_map/while/body/eval_jaxpr/ppermute | solution.py:61
  258.7 14.4 %conditional.2 = (bf16[128,1024]{1,0:T(8,128)(2,1)S(1)}) conditional(s32[]{:T(128)} %convert_element_type.85, bf16[128,1024]{1,0:T(8,128)(2,1)S(1)} %bitcast_select_fusion.4, (bf16[128,1024]{1,0:T(8,128)(2,1)S(1)}, f32[1,1024]{1,0:T(1,128)S(1)}, bf16[1024,4096]{1,0:T(8,128)(2,1)}, s32[8]{0:T(128)S(1)}, s32[]{:T(128)}, ...), branch_computations={%region_4.4_spmd, %region_5.9_spmd} | conditional | flops 1416003968 | bytes 24954192 | solution.py:162
  259.1 4.8 %multiply_convert_fusion = bf16[128,4096]{1,0:T(8,128)(2,1)S(1)} fusion(bf16[1024,4096]{1,0:T(8,128)(2,1)} %get-tuple-element.315, bf16[128,1024]{1,0:T(8,128)(2,1)S(1)} %get-tuple-element.313, f32[1024]{0:T(1024)S(1)} %bitcast.83, f32[128]{0:T(128)S(1)} %add_rsqrt_fusion.1, f32[128]{0:T(128)S(1)} %broadcast_multiply_fusion.1), kind=kOutput, calls=%fused_computation.2 | convolution fusion | flops 1077018624 | bytes 9704448 | tf_op jit(solution)/shard_map/while/body/eval_jaxpr/cond/branch_1_fun/dot_general | solution.py:73
  273.1 1.9 collective-permute-start
  275.1 1.7 fusion.50
  276.8 4.0 collective-permute-done
  281.8 14.4 %conditional.2 = (bf16[128,1024]{1,0:T(8,128)(2,1)S(1)}) conditional(s32[]{:T(128)} %convert_element_type.85, bf16[128,1024]{1,0:T(8,128)(2,1)S(1)} %bitcast_select_fusion.4, (bf16[128,1024]{1,0:T(8,128)(2,1)S(1)}, f32[1,1024]{1,0:T(1,128)S(1)}, bf16[1024,4096]{1,0:T(8,128)(2,1)}, s32[8]{0:T(128)S(1)}, s32[]{:T(128)}, ...), branch_computations={%region_4.4_spmd, %region_5.9_spmd} | conditional | flops 1416003968 | bytes 24954192 | solution.py:162
  282.2 4.8 %multiply_convert_fusion = bf16[128,4096]{1,0:T(8,128)(2,1)S(1)} fusion(bf16[1024,4096]{1,0:T(8,128)(2,1)} %get-tuple-element.315, bf16[128,1024]{1,0:T(8,128)(2,1)S(1)} %get-tuple-element.313, f32[1024]{0:T(1024)S(1)} %bitcast.83, f32[128]{0:T(128)S(1)} %add_rsqrt_fusion.1, f32[128]{0:T(128)S(1)} %broadcast_multiply_fusion.1), kind=kOutput, calls=%fused_computation.2 | convolution fusion | flops 1077018624 | bytes 9704448 | tf_op jit(solution)/shard_map/while/body/eval_jaxpr/cond/branch_1_fun/dot_general | solution.py:73
  296.2 1.9 collective-permute-start
  299.9 4.0 collective-permute-done
  304.9 14.4 %conditional.2 = (bf16[128,1024]{1,0:T(8,128)(2,1)S(1)}) conditional(s32[]{:T(128)} %convert_element_type.85, bf16[128,1024]{1,0:T(8,128)(2,1)S(1)} %bitcast_select_fusion.4, (bf16[128,1024]{1,0:T(8,128)(2,1)S(1)}, f32[1,1024]{1,0:T(1,128)S(1)}, bf16[1024,4096]{1,0:T(8,128)(2,1)}, s32[8]{0:T(128)S(1)}, s32[]{:T(128)}, ...), branch_computations={%region_4.4_spmd, %region_5.9_spmd} | conditional | flops 1416003968 | bytes 24954192 | solution.py:162
  305.3 4.8 %multiply_convert_fusion = bf16[128,4096]{1,0:T(8,128)(2,1)S(1)} fusion(bf16[1024,4096]{1,0:T(8,128)(2,1)} %get-tuple-element.315, bf16[128,1024]{1,0:T(8,128)(2,1)S(1)} %get-tuple-element.313, f32[1024]{0:T(1024)S(1)} %bitcast.83, f32[128]{0:T(128)S(1)} %add_rsqrt_fusion.1, f32[128]{0:T(128)S(1)} %broadcast_multiply_fusion.1), kind=kOutput, calls=%fused_computation.2 | convolution fusion | flops 1077018624 | bytes 9704448 | tf_op jit(solution)/shard_map/while/body/eval_jaxpr/cond/branch_1_fun/dot_general | solution.py:73
  319.3 1.9 collective-permute-start
  321.2 1.7 fusion.50
  322.9 4.0 collective-permute-done
  328.0 14.4 %conditional.2 = (bf16[128,1024]{1,0:T(8,128)(2,1)S(1)}) conditional(s32[]{:T(128)} %convert_element_type.85, bf16[128,1024]{1,0:T(8,128)(2,1)S(1)} %bitcast_select_fusion.4, (bf16[128,1024]{1,0:T(8,128)(2,1)S(1)}, f32[1,1024]{1,0:T(1,128)S(1)}, bf16[1024,4096]{1,0:T(8,128)(2,1)}, s32[8]{0:T(128)S(1)}, s32[]{:T(128)}, ...), branch_computations={%region_4.4_spmd, %region_5.9_spmd} | conditional | flops 1416003968 | bytes 24954192 | solution.py:162
  328.3 4.8 %multiply_convert_fusion = bf16[128,4096]{1,0:T(8,128)(2,1)S(1)} fusion(bf16[1024,4096]{1,0:T(8,128)(2,1)} %get-tuple-element.315, bf16[128,1024]{1,0:T(8,128)(2,1)S(1)} %get-tuple-element.313, f32[1024]{0:T(1024)S(1)} %bitcast.83, f32[128]{0:T(128)S(1)} %add_rsqrt_fusion.1, f32[128]{0:T(128)S(1)} %broadcast_multiply_fusion.1), kind=kOutput, calls=%fused_computation.2 | convolution fusion | flops 1077018624 | bytes 9704448 | tf_op jit(solution)/shard_map/while/body/eval_jaxpr/cond/branch_1_fun/dot_general | solution.py:73
  342.4 1.9 collective-permute-start
  344.3 1.7 fusion.50
  346.0 4.0 collective-permute-done
  351.0 14.4 %conditional.2 = (bf16[128,1024]{1,0:T(8,128)(2,1)S(1)}) conditional(s32[]{:T(128)} %convert_element_type.85, bf16[128,1024]{1,0:T(8,128)(2,1)S(1)} %bitcast_select_fusion.4, (bf16[128,1024]{1,0:T(8,128)(2,1)S(1)}, f32[1,1024]{1,0:T(1,128)S(1)}, bf16[1024,4096]{1,0:T(8,128)(2,1)}, s32[8]{0:T(128)S(1)}, s32[]{:T(128)}, ...), branch_computations={%region_4.4_spmd, %region_5.9_spmd} | conditional | flops 1416003968 | bytes 24954192 | solution.py:162
  351.4 4.8 %multiply_convert_fusion = bf16[128,4096]{1,0:T(8,128)(2,1)S(1)} fusion(bf16[1024,4096]{1,0:T(8,128)(2,1)} %get-tuple-element.315, bf16[128,1024]{1,0:T(8,128)(2,1)S(1)} %get-tuple-element.313, f32[1024]{0:T(1024)S(1)} %bitcast.83, f32[128]{0:T(128)S(1)} %add_rsqrt_fusion.1, f32[128]{0:T(128)S(1)} %broadcast_multiply_fusion.1), kind=kOutput, calls=%fused_computation.2 | convolution fusion | flops 1077018624 | bytes 9704448 | tf_op jit(solution)/shard_map/while/body/eval_jaxpr/cond/branch_1_fun/dot_general | solution.py:73
  365.4 1.9 collective-permute-start
  369.1 4.0 collective-permute-done
  374.1 14.4 %conditional.2 = (bf16[128,1024]{1,0:T(8,128)(2,1)S(1)}) conditional(s32[]{:T(128)} %convert_element_type.85, bf16[128,1024]{1,0:T(8,128)(2,1)S(1)} %bitcast_select_fusion.4, (bf16[128,1024]{1,0:T(8,128)(2,1)S(1)}, f32[1,1024]{1,0:T(1,128)S(1)}, bf16[1024,4096]{1,0:T(8,128)(2,1)}, s32[8]{0:T(128)S(1)}, s32[]{:T(128)}, ...), branch_computations={%region_4.4_spmd, %region_5.9_spmd} | conditional | flops 1416003968 | bytes 24954192 | solution.py:162
  374.5 4.8 %multiply_convert_fusion = bf16[128,4096]{1,0:T(8,128)(2,1)S(1)} fusion(bf16[1024,4096]{1,0:T(8,128)(2,1)} %get-tuple-element.315, bf16[128,1024]{1,0:T(8,128)(2,1)S(1)} %get-tuple-element.313, f32[1024]{0:T(1024)S(1)} %bitcast.83, f32[128]{0:T(128)S(1)} %add_rsqrt_fusion.1, f32[128]{0:T(128)S(1)} %broadcast_multiply_fusion.1), kind=kOutput, calls=%fused_computation.2 | convolution fusion | flops 1077018624 | bytes 9704448 | tf_op jit(solution)/shard_map/while/body/eval_jaxpr/cond/branch_1_fun/dot_general | solution.py:73
  388.5 1.9 collective-permute-start
  392.2 4.0 collective-permute-done
  397.2 14.4 %conditional.2 = (bf16[128,1024]{1,0:T(8,128)(2,1)S(1)}) conditional(s32[]{:T(128)} %convert_element_type.85, bf16[128,1024]{1,0:T(8,128)(2,1)S(1)} %bitcast_select_fusion.4, (bf16[128,1024]{1,0:T(8,128)(2,1)S(1)}, f32[1,1024]{1,0:T(1,128)S(1)}, bf16[1024,4096]{1,0:T(8,128)(2,1)}, s32[8]{0:T(128)S(1)}, s32[]{:T(128)}, ...), branch_computations={%region_4.4_spmd, %region_5.9_spmd} | conditional | flops 1416003968 | bytes 24954192 | solution.py:162
  397.5 4.8 %multiply_convert_fusion = bf16[128,4096]{1,0:T(8,128)(2,1)S(1)} fusion(bf16[1024,4096]{1,0:T(8,128)(2,1)} %get-tuple-element.315, bf16[128,1024]{1,0:T(8,128)(2,1)S(1)} %get-tuple-element.313, f32[1024]{0:T(1024)S(1)} %bitcast.83, f32[128]{0:T(128)S(1)} %add_rsqrt_fusion.1, f32[128]{0:T(128)S(1)} %broadcast_multiply_fusion.1), kind=kOutput, calls=%fused_computation.2 | convolution fusion | flops 1077018624 | bytes 9704448 | tf_op jit(solution)/shard_map/while/body/eval_jaxpr/cond/branch_1_fun/dot_general | solution.py:73
  411.6 1.9 collective-permute-start
  415.2 4.0 collective-permute-done
  420.2 14.4 %conditional.2 = (bf16[128,1024]{1,0:T(8,128)(2,1)S(1)}) conditional(s32[]{:T(128)} %convert_element_type.85, bf16[128,1024]{1,0:T(8,128)(2,1)S(1)} %bitcast_select_fusion.4, (bf16[128,1024]{1,0:T(8,128)(2,1)S(1)}, f32[1,1024]{1,0:T(1,128)S(1)}, bf16[1024,4096]{1,0:T(8,128)(2,1)}, s32[8]{0:T(128)S(1)}, s32[]{:T(128)}, ...), branch_computations={%region_4.4_spmd, %region_5.9_spmd} | conditional | flops 1416003968 | bytes 24954192 | solution.py:162
  420.6 4.8 %multiply_convert_fusion = bf16[128,4096]{1,0:T(8,128)(2,1)S(1)} fusion(bf16[1024,4096]{1,0:T(8,128)(2,1)} %get-tuple-element.315, bf16[128,1024]{1,0:T(8,128)(2,1)S(1)} %get-tuple-element.313, f32[1024]{0:T(1024)S(1)} %bitcast.83, f32[128]{0:T(128)S(1)} %add_rsqrt_fusion.1, f32[128]{0:T(128)S(1)} %broadcast_multiply_fusion.1), kind=kOutput, calls=%fused_computation.2 | convolution fusion | flops 1077018624 | bytes 9704448 | tf_op jit(solution)/shard_map/while/body/eval_jaxpr/cond/branch_1_fun/dot_general | solution.py:73
  434.6 1.9 collective-permute-start
  438.3 4.0 collective-permute-done
  443.3 12.0 %collective-permute-start = (bf16[128,1024]{1,0:T(8,128)(2,1)S(1)}, bf16[128,1024]{1,0:T(8,128)(2,1)S(1)}, u32[]{:S(2)}, u32[]{:S(2)}) collective-permute-start(bf16[128,1024]{1,0:T(8,128)(2,1)S(1)} %get-tuple-element.475), channel_id=1, source_target_pairs={{0,32},{32,64},{64,96},{96,128},{128,160},{160,192},{192,224},{1,3... | collective-permute-start | bytes 786440 | tf_op jit(solution)/shard_map/while/body/eval_jaxpr/ppermute | solution.py:61
  (217 shorter events, 110.6 us)
Async XLA Ops:
  6.5 30.9 %copy-start = (bf16[256,1024]{1,0:T(8,128)(2,1)S(1)}, bf16[256,1024]{1,0:T(8,128)(2,1)}, u32[]{:S(2)}) copy-start(bf16[256,1024]{1,0:T(8,128)(2,1)} %param.15) | copy-start | bytes 1572868
  6.5 119.3 %all-gather.2.cloned.1.call-start = ((), (), s32[]{:S(2)}) async-start(), calls=%async_computation.4 | async-start | bytes 10813440 | tf_op jit(solution)/shard_map/all_gather | solution.py:45
  38.6 4.9 %copy-start.4 = (s32[1,1,128,1]{2,3,1,0:T(1,128)S(1)}, s32[1,1,128,1]{2,3,1,0:T(1,128)}, u32[]{:S(2)}) copy-start(s32[1,1,128,1]{2,3,1,0:T(1,128)} %param.12) | copy-start | bytes 1540
  39.5 21.7 %all-to-all-start.2 = ((bf16[32,8,1024]{2,1,0:T(8,128)(2,1)}), bf16[32,8,1024]{2,1,0:T(8,128)(2,1)S(1)}, u32[]{:S(2)}, u32[]{:S(2)}) async-start(bf16[32,8,1024]{2,1,0:T(8,128)(2,1)} %fusion.37), calls=%async_computation.2 | async-start | bytes 1048576 | tf_op jit(solution)/shard_map/all_to_all | solution.py:119
  63.8 71.6 %all-to-all-start.3 = ((bf16[8,1,128,1024]{3,2,1,0:T(8,128)(2,1)}), bf16[8,1,128,1024]{3,2,1,0:T(8,128)(2,1)}, u32[]{:S(2)}, u32[]{:S(2)}) async-start(bf16[8,1,128,1024]{3,2,1,0:T(8,128)(2,1)} %broadcast_in_dim.94), calls=%async_computation.3 | async-start | bytes 4194304 | tf_op jit(solution)/shard_map/all_to_all | solution.py:50
  135.4 1.6 copy-start.3
  135.4 1.6 copy-start.5
  135.4 1.6 copy-start.6
  138.1 7.7 %collective-permute-start = (bf16[128,1024]{1,0:T(8,128)(2,1)S(1)}, bf16[128,1024]{1,0:T(8,128)(2,1)S(1)}, u32[]{:S(2)}, u32[]{:S(2)}) collective-permute-start(bf16[128,1024]{1,0:T(8,128)(2,1)S(1)} %get-tuple-element.475), channel_id=1, source_target_pairs={{0,32},{32,64},{64,96},{96,128},{128,160},{160,192},{192,224},{1,3... | collective-permute-start | bytes 786440 | tf_op jit(solution)/shard_map/while/body/eval_jaxpr/ppermute | solution.py:61
  146.8 7.7 %collective-permute-start = (bf16[128,1024]{1,0:T(8,128)(2,1)S(1)}, bf16[128,1024]{1,0:T(8,128)(2,1)S(1)}, u32[]{:S(2)}, u32[]{:S(2)}) collective-permute-start(bf16[128,1024]{1,0:T(8,128)(2,1)S(1)} %get-tuple-element.475), channel_id=1, source_target_pairs={{0,32},{32,64},{64,96},{96,128},{128,160},{160,192},{192,224},{1,3... | collective-permute-start | bytes 786440 | tf_op jit(solution)/shard_map/while/body/eval_jaxpr/ppermute | solution.py:61
  155.5 7.7 %collective-permute-start = (bf16[128,1024]{1,0:T(8,128)(2,1)S(1)}, bf16[128,1024]{1,0:T(8,128)(2,1)S(1)}, u32[]{:S(2)}, u32[]{:S(2)}) collective-permute-start(bf16[128,1024]{1,0:T(8,128)(2,1)S(1)} %get-tuple-element.475), channel_id=1, source_target_pairs={{0,32},{32,64},{64,96},{96,128},{128,160},{160,192},{192,224},{1,3... | collective-permute-start | bytes 786440 | tf_op jit(solution)/shard_map/while/body/eval_jaxpr/ppermute | solution.py:61
  164.2 7.7 %collective-permute-start = (bf16[128,1024]{1,0:T(8,128)(2,1)S(1)}, bf16[128,1024]{1,0:T(8,128)(2,1)S(1)}, u32[]{:S(2)}, u32[]{:S(2)}) collective-permute-start(bf16[128,1024]{1,0:T(8,128)(2,1)S(1)} %get-tuple-element.475), channel_id=1, source_target_pairs={{0,32},{32,64},{64,96},{96,128},{128,160},{160,192},{192,224},{1,3... | collective-permute-start | bytes 786440 | tf_op jit(solution)/shard_map/while/body/eval_jaxpr/ppermute | solution.py:61
  172.9 7.7 %collective-permute-start = (bf16[128,1024]{1,0:T(8,128)(2,1)S(1)}, bf16[128,1024]{1,0:T(8,128)(2,1)S(1)}, u32[]{:S(2)}, u32[]{:S(2)}) collective-permute-start(bf16[128,1024]{1,0:T(8,128)(2,1)S(1)} %get-tuple-element.475), channel_id=1, source_target_pairs={{0,32},{32,64},{64,96},{96,128},{128,160},{160,192},{192,224},{1,3... | collective-permute-start | bytes 786440 | tf_op jit(solution)/shard_map/while/body/eval_jaxpr/ppermute | solution.py:61
  181.6 76.2 %collective-permute-start = (bf16[128,1024]{1,0:T(8,128)(2,1)S(1)}, bf16[128,1024]{1,0:T(8,128)(2,1)S(1)}, u32[]{:S(2)}, u32[]{:S(2)}) collective-permute-start(bf16[128,1024]{1,0:T(8,128)(2,1)S(1)} %get-tuple-element.475), channel_id=1, source_target_pairs={{0,32},{32,64},{64,96},{96,128},{128,160},{160,192},{192,224},{1,3... | collective-permute-start | bytes 786440 | tf_op jit(solution)/shard_map/while/body/eval_jaxpr/ppermute | solution.py:61
  263.9 1.0 copy-start.2
  269.6 0.8 copy-start.1
  273.1 7.7 %collective-permute-start = (bf16[128,1024]{1,0:T(8,128)(2,1)S(1)}, bf16[128,1024]{1,0:T(8,128)(2,1)S(1)}, u32[]{:S(2)}, u32[]{:S(2)}) collective-permute-start(bf16[128,1024]{1,0:T(8,128)(2,1)S(1)} %get-tuple-element.475), channel_id=1, source_target_pairs={{0,32},{32,64},{64,96},{96,128},{128,160},{160,192},{192,224},{1,3... | collective-permute-start | bytes 786440 | tf_op jit(solution)/shard_map/while/body/eval_jaxpr/ppermute | solution.py:61
  287.0 1.0 copy-start.2
  292.7 0.8 copy-start.1
  296.2 7.7 %collective-permute-start = (bf16[128,1024]{1,0:T(8,128)(2,1)S(1)}, bf16[128,1024]{1,0:T(8,128)(2,1)S(1)}, u32[]{:S(2)}, u32[]{:S(2)}) collective-permute-start(bf16[128,1024]{1,0:T(8,128)(2,1)S(1)} %get-tuple-element.475), channel_id=1, source_target_pairs={{0,32},{32,64},{64,96},{96,128},{128,160},{160,192},{192,224},{1,3... | collective-permute-start | bytes 786440 | tf_op jit(solution)/shard_map/while/body/eval_jaxpr/ppermute | solution.py:61
  310.1 1.0 copy-start.2
  315.8 0.8 copy-start.1
  319.3 7.7 %collective-permute-start = (bf16[128,1024]{1,0:T(8,128)(2,1)S(1)}, bf16[128,1024]{1,0:T(8,128)(2,1)S(1)}, u32[]{:S(2)}, u32[]{:S(2)}) collective-permute-start(bf16[128,1024]{1,0:T(8,128)(2,1)S(1)} %get-tuple-element.475), channel_id=1, source_target_pairs={{0,32},{32,64},{64,96},{96,128},{128,160},{160,192},{192,224},{1,3... | collective-permute-start | bytes 786440 | tf_op jit(solution)/shard_map/while/body/eval_jaxpr/ppermute | solution.py:61
  333.2 1.0 copy-start.2
  338.8 0.8 copy-start.1
  342.4 7.7 %collective-permute-start = (bf16[128,1024]{1,0:T(8,128)(2,1)S(1)}, bf16[128,1024]{1,0:T(8,128)(2,1)S(1)}, u32[]{:S(2)}, u32[]{:S(2)}) collective-permute-start(bf16[128,1024]{1,0:T(8,128)(2,1)S(1)} %get-tuple-element.475), channel_id=1, source_target_pairs={{0,32},{32,64},{64,96},{96,128},{128,160},{160,192},{192,224},{1,3... | collective-permute-start | bytes 786440 | tf_op jit(solution)/shard_map/while/body/eval_jaxpr/ppermute | solution.py:61
  356.2 1.0 copy-start.2
  361.9 0.8 copy-start.1
  365.4 7.7 %collective-permute-start = (bf16[128,1024]{1,0:T(8,128)(2,1)S(1)}, bf16[128,1024]{1,0:T(8,128)(2,1)S(1)}, u32[]{:S(2)}, u32[]{:S(2)}) collective-permute-start(bf16[128,1024]{1,0:T(8,128)(2,1)S(1)} %get-tuple-element.475), channel_id=1, source_target_pairs={{0,32},{32,64},{64,96},{96,128},{128,160},{160,192},{192,224},{1,3... | collective-permute-start | bytes 786440 | tf_op jit(solution)/shard_map/while/body/eval_jaxpr/ppermute | solution.py:61
  379.3 1.0 copy-start.2
  385.0 0.8 copy-start.1
  388.5 7.7 %collective-permute-start = (bf16[128,1024]{1,0:T(8,128)(2,1)S(1)}, bf16[128,1024]{1,0:T(8,128)(2,1)S(1)}, u32[]{:S(2)}, u32[]{:S(2)}) collective-permute-start(bf16[128,1024]{1,0:T(8,128)(2,1)S(1)} %get-tuple-element.475), channel_id=1, source_target_pairs={{0,32},{32,64},{64,96},{96,128},{128,160},{160,192},{192,224},{1,3... | collective-permute-start | bytes 786440 | tf_op jit(solution)/shard_map/while/body/eval_jaxpr/ppermute | solution.py:61
  402.4 1.0 copy-start.2
  408.0 0.8 copy-start.1
  411.6 7.7 %collective-permute-start = (bf16[128,1024]{1,0:T(8,128)(2,1)S(1)}, bf16[128,1024]{1,0:T(8,128)(2,1)S(1)}, u32[]{:S(2)}, u32[]{:S(2)}) collective-permute-start(bf16[128,1024]{1,0:T(8,128)(2,1)S(1)} %get-tuple-element.475), channel_id=1, source_target_pairs={{0,32},{32,64},{64,96},{96,128},{128,160},{160,192},{192,224},{1,3... | collective-permute-start | bytes 786440 | tf_op jit(solution)/shard_map/while/body/eval_jaxpr/ppermute | solution.py:61
  425.4 1.0 copy-start.2
  431.1 0.8 copy-start.1
  434.6 7.7 %collective-permute-start = (bf16[128,1024]{1,0:T(8,128)(2,1)S(1)}, bf16[128,1024]{1,0:T(8,128)(2,1)S(1)}, u32[]{:S(2)}, u32[]{:S(2)}) collective-permute-start(bf16[128,1024]{1,0:T(8,128)(2,1)S(1)} %get-tuple-element.475), channel_id=1, source_target_pairs={{0,32},{32,64},{64,96},{96,128},{128,160},{160,192},{192,224},{1,3... | collective-permute-start | bytes 786440 | tf_op jit(solution)/shard_map/while/body/eval_jaxpr/ppermute | solution.py:61
  443.3 13.8 %collective-permute-start = (bf16[128,1024]{1,0:T(8,128)(2,1)S(1)}, bf16[128,1024]{1,0:T(8,128)(2,1)S(1)}, u32[]{:S(2)}, u32[]{:S(2)}) collective-permute-start(bf16[128,1024]{1,0:T(8,128)(2,1)S(1)} %get-tuple-element.475), channel_id=1, source_target_pairs={{0,32},{32,64},{64,96},{96,128},{128,160},{160,192},{192,224},{1,3... | collective-permute-start | bytes 786440 | tf_op jit(solution)/shard_map/while/body/eval_jaxpr/ppermute | solution.py:61
Sparse Core Ops, SparseCore 0:
  9.9 115.8 all-gather.1
where the time goes:
time: 467 us; the launch traced here: 464 us
  waiting for transfers between devices  200 us (43%)
  matrix products  63.5 us (14%)
  local copies, waits for them, and re-layouts  56.7 us (12%)
  other arithmetic  55.8 us (12%)
  starting transfers between devices  47.6 us (10%)
  blocking collectives  25.8 us (6%)
  between operations  13.5 us (3%)
    ppermute x15, waiting for transfers between devices, from_behind(): return lax.ppermute(block, axis, route)  125 us
    all_gather x1, waiting for transfers between devices, side_by_side(): lax.all_gather(both, axis, axis=dim, tiled=True)  57.2 us
    ppermute x15, starting transfers between devices, from_behind(): return lax.ppermute(block, axis, route)  38.9 us
    dot_general x8, matrix products, layer_part(): jnp.dot(normed, weight_in, preferred_element_type=jnp.float32)  38.6 us
    dynamic_update_slice x15, other arithmetic, tick(): lax.dynamic_update_slice(saved, jnp.where(valid, finished[None], previous...  25.9 us
    all_to_all x2, blocking collectives, moved_by_axis(): out = lax.all_to_all(out, axes[k], k, k, tiled=True)  25.8 us
    cond x40, local copies, waits for them, and re-layouts  20 us
    all_to_all x1, waiting for transfers between devices, lookup_items(): lax.all_to_all(found, DP, split_axis=0, concat_axis=0, tiled=True)  17.8 us
  transfers between devices with their start and end apart: 18, of which 16 were waited for; matrix products, arithmetic and copies ran while one was open for 9% of the time, Pallas kernels for 0%

commit v1 on v0

v1 whole, which is shorter than its diff:
```python
import functools

import jax
import jax.numpy as jnp
from jax import lax
from jax.experimental import pallas as pl
from jax.experimental.pallas import tpu as pltpu
from jax.sharding import Mesh
from jax.sharding import PartitionSpec as P

HEADS = 8
HEAD = 128
WIDTH = 1024
ROWS = 128
PAIR = 2 * HEAD
EPS = 1e-05
STAGES = 4
SHARE = 4
DP = ("dp_0", "dp_1")
ALL = ("chip", "core")


def silu(values):
    half = 0.5 * values
    return half + half * jnp.tanh(half)


def normalize(values):
    center = values - jnp.mean(values, axis=-1, keepdims=True)
    spread = jnp.mean(center * center, axis=-1, keepdims=True)
    return center * lax.rsqrt(spread + EPS)


def stage_kernel(
    step_ref,
    info_ref,
    inputs_ref,
    incoming_ref,
    mine_ref,
    other_ref,
    gain_in_ref,
    gain_mid_ref,
    out_in,
    send_in,
    out_ref,
    send_ref,
    next_ref,
    weights,
    current,
    projected,
    results,
    weight_sems,
    out_sem,
    in_sem,
):
    core = info_ref[8]
    chip = info_ref[9]
    which = step_ref[0] - 2 * chip
    pairs = HEADS // 2

    def columns(part):
        if part == pairs:
            return [pl.ds(4 * WIDTH, WIDTH)]
        return [pl.ds(block * WIDTH + part * PAIR, PAIR) for block in range(4)]

    def fetch(source, section, part):
        return [
            pltpu.make_async_copy(
                source.at[:, cols], weights.at[section, :, cols], weight_sems.at[section, part, k]
            )
            for k, cols in enumerate(columns(part))
        ]

    @pl.when((which >= 0) & (which < SHARE))
    def _():
        @pl.when(chip == 0)
        def _():
            pltpu.make_async_copy(inputs_ref.at[which], current, in_sem).start()

        @pl.when(chip != 0)
        def _():
            pltpu.make_async_copy(incoming_ref, current, in_sem).start()

        for section in range(2):

            @pl.when(core == section)
            def _():
                for part in range(pairs + 1):
                    for copy in fetch(mine_ref, section, part):
                        copy.start()

            @pl.when(core != section)
            def _():
                for part in range(pairs + 1):
                    for copy in fetch(other_ref, section, part):
                        copy.start()

        length = info_ref[2 * which + core]
        row = lax.broadcasted_iota(jnp.int32, (ROWS, ROWS), 0)
        col = lax.broadcasted_iota(jnp.int32, (ROWS, ROWS), 1)
        allowed = (col <= row) & (col < length)
        pltpu.make_async_copy(incoming_ref, current, in_sem).wait()

        for section in range(2):
            block = current[...] if section == 0 else results[0]
            wide = block.astype(jnp.float32)
            normed = (normalize(wide) * gain_in_ref[pl.ds(section, 1), :]).astype(jnp.bfloat16)
            heads = []
            for part in range(pairs):
                for copy in fetch(mine_ref, section, part):
                    copy.wait()
                q_k_v = []
                for index in (2, 3, 1, 0):
                    cols = columns(part)[index]
                    value = silu(
                        jnp.dot(
                            normed,
                            weights[section, :, cols],
                            preferred_element_type=jnp.float32,
                        )
                    ).astype(jnp.bfloat16)
                    if index == 0:
                        projected[:, pl.ds(part * PAIR, PAIR)] = value
                    else:
                        q_k_v.append(value)
                queries, keys, values = q_k_v
                for head in range(2):
                    at = slice(head * HEAD, (head + 1) * HEAD)
                    scores = lax.dot_general(
                        queries[:, at],
                        keys[:, at],
                        (((1,), (1,)), ((), ())),
                        preferred_element_type=jnp.float32,
                    )
                    weight = jnp.where(allowed, silu(scores * (HEAD**-0.5)), 0.0)
                    heads.append(
                        jnp.dot(
                            weight.astype(jnp.bfloat16),
                            values[:, at],
                            preferred_element_type=jnp.float32,
                        )
                    )
            attn = jnp.concatenate(heads, axis=1)
            mixed = normalize(attn) * gain_mid_ref[pl.ds(section, 1), :]
            mixed = (mixed * projected[...].astype(jnp.float32)).astype(jnp.bfloat16)
            for copy in fetch(mine_ref, section, pairs):
                copy.wait()
            result = jnp.dot(
                mixed,
                weights[section, :, pl.ds(4 * WIDTH, WIDTH)],
                preferred_element_type=jnp.float32,
            )
            result = (result + wide).astype(jnp.bfloat16)
            results[section] = result
            if section == 1:
                next_ref[...] = result

            @pl.when(core == section)
            def _():
                pltpu.make_async_copy(
                    results.at[section], out_ref.at[2 * which + core], out_sem.at[section]
                ).start()

            @pl.when(core != section)
            def _():
                pltpu.make_async_copy(
                    results.at[section], send_ref.at[which], out_sem.at[section]
                ).start()

        for section in range(2):
            pltpu.make_async_copy(
                results.at[section], send_ref.at[which], out_sem.at[section]
            ).wait()


def stage(step, info, inputs, incoming, mine, other, gain_in, gain_mid, out, send):
    smem = pl.BlockSpec(memory_space=pltpu.SMEM)
    vmem = pl.BlockSpec(memory_space=pltpu.VMEM)
    anywhere = pl.BlockSpec(memory_space=pl.ANY)
    block = jax.ShapeDtypeStruct((ROWS, WIDTH), jnp.bfloat16)
    return pl.pallas_call(
        stage_kernel,
        out_shape=(
            jax.ShapeDtypeStruct(out.shape, out.dtype),
            jax.ShapeDtypeStruct(send.shape, send.dtype),
            block,
        ),
        in_specs=[smem, smem, anywhere, anywhere, anywhere, anywhere, vmem, vmem, anywhere, anywhere],
        out_specs=(anywhere, anywhere, vmem),
        scratch_shapes=[
            pltpu.VMEM((2, WIDTH, 5 * WIDTH), jnp.bfloat16),
            pltpu.VMEM((ROWS, WIDTH), jnp.bfloat16),
            pltpu.VMEM((ROWS, WIDTH), jnp.bfloat16),
            pltpu.VMEM((2, ROWS, WIDTH), jnp.bfloat16),
            pltpu.SemaphoreType.DMA((2, HEADS // 2 + 1, 4)),
            pltpu.SemaphoreType.DMA((2,)),
            pltpu.SemaphoreType.DMA,
        ],
        input_output_aliases={8: 0, 9: 1},
        compiler_params=pltpu.CompilerParams(vmem_limit_bytes=40 * 1024 * 1024),
        cost_estimate=pl.CostEstimate(
            flops=2 * 2 * ROWS * WIDTH * 5 * WIDTH,
            bytes_accessed=2 * 2 * WIDTH * 5 * WIDTH,
            transcendentals=2 * ROWS * 5 * WIDTH,
        ),
    )(step, info, inputs, incoming, mine, other, gain_in, gain_mid, out, send)


def place_kernel(info_ref, received, out_in, out_ref, sems):
    core = info_ref[8]
    copies = [
        pltpu.make_async_copy(received.at[j], out_ref.at[2 * j + 1 - core], sems.at[j])
        for j in range(SHARE)
    ]
    for copy in copies:
        copy.start()
    for copy in copies:
        copy.wait()


def place(info, received, out):
    return pl.pallas_call(
        place_kernel,
        out_shape=jax.ShapeDtypeStruct(out.shape, out.dtype),
        in_specs=[
            pl.BlockSpec(memory_space=pltpu.SMEM),
            pl.BlockSpec(memory_space=pltpu.VMEM),
            pl.BlockSpec(memory_space=pl.ANY),
        ],
        out_specs=pl.BlockSpec(memory_space=pl.ANY),
        scratch_shapes=[pltpu.SemaphoreType.DMA((SHARE,))],
        input_output_aliases={2: 0},
        compiler_params=pltpu.CompilerParams(vmem_limit_bytes=8 * 1024 * 1024),
    )(info, received, out)


def lookup_items(item_owner, item_row, table):
    groups = lax.axis_size(DP)
    owner = item_owner.reshape(-1)
    rows = item_row.reshape(-1)
    seq_len = rows.shape[0]
    slots_each = max(2, 2 * seq_len // groups)
    match = (owner[:, None] == jnp.arange(groups, dtype=jnp.int32)[None, :]).astype(jnp.int32)
    earlier = jnp.cumsum(match, axis=0) - match
    slot = jnp.sum(earlier * match, axis=1)
    placed = match[:, :, None] * (
        slot[:, None, None] == jnp.arange(slots_each, dtype=jnp.int32)[None, None, :]
    ).astype(jnp.int32)
    request = jnp.sum(placed * rows[:, None, None], axis=0)
    received = lax.all_to_all(request, DP, split_axis=0, concat_axis=0, tiled=True)
    found = jnp.take(table, received.reshape(-1), axis=0, mode="clip")
    answered = lax.all_to_all(
        found.reshape(groups, slots_each, -1), DP, split_axis=0, concat_axis=0, tiled=True
    )
    flat_rows = answered.reshape(groups * slots_each, table.shape[1])
    return jnp.take(flat_rows, owner * slots_each + slot, axis=0, mode="clip")


def swap(block):
    return lax.ppermute(block, "core", [(0, 1), (1, 0)])


def on_device(item_owner, item_row, lengths, table, w_in, w_out, gain_in, gain_mid):
    core = lax.axis_index("core")
    chip = lax.axis_index("chip")
    shard = jnp.concatenate([w_in[0], w_out[0]], axis=1)
    mine = lax.all_gather(shard, DP, axis=0, tiled=True)
    embedded = lookup_items(item_owner, item_row, table)
    inputs = jnp.stack(
        [embedded] + [lax.ppermute(embedded, "chip", [(k, 0)]) for k in range(1, STAGES)]
    )
    gains = jnp.concatenate([gain_in, gain_mid], axis=0)
    gains_other = swap(gains)
    first = jnp.where(core == 0, gains, gains_other)
    second = jnp.where(core == 0, gains_other, gains)
    scale_in = jnp.stack([first[0], second[0]])
    scale_mid = jnp.stack([first[1], second[1]])
    other = swap(mine)
    info = jnp.concatenate(
        [lengths[:, 0], jnp.stack([core, chip]).astype(jnp.int32), jnp.zeros((6,), jnp.int32)]
    )
    blank = jnp.zeros((ROWS, WIDTH), jnp.bfloat16)
    out = jnp.zeros((2 * SHARE, ROWS, WIDTH), jnp.bfloat16)
    send = jnp.zeros((SHARE, ROWS, WIDTH), jnp.bfloat16)
    steps = SHARE + 2 * (STAGES - 1)
    forward = [(i, i + 1) for i in range(STAGES - 1)]

    def body(step, carry):
        out, send, previous, incoming = carry
        arriving = lax.ppermute(previous, "chip", forward)
        out, send, result = stage(
            step.reshape(1), info, inputs, incoming, mine, other, scale_in, scale_mid, out, send
        )
        return (out, send, result, arriving)

    out, send, _, _ = lax.fori_loop(0, steps, body, (out, send, blank, blank))
    out = place(info, swap(send), out)
    return out[None, None]


def solution(mesh):
    split = Mesh(mesh.devices.reshape(STAGES, 2, 4, 8), ("chip", "core", "dp_0", "dp_1"))
    placed = (
        P(ALL, DP, None, None),
        P(ALL, DP, None),
        P(None, DP),
        P(DP, None),
        P(ALL, DP, None),
        P(ALL, DP, None),
        P(ALL, None),
        P(ALL, None),
    )
    return jax.shard_map(
        on_device,
        mesh=split,
        in_specs=placed,
        out_specs=P(ALL, DP, None, None, None),
        check_vma=False,
    )
```

time: 467 us -> 312 us (0.67)
  matrix products: 63.5 us -> 0 us
  other arithmetic: 55.8 us -> 6.75 us
  Pallas kernels: 0 us -> 47.6 us
  local copies, waits for them, and re-layouts: 56.7 us -> 15.9 us
  starting transfers between devices: 47.6 us -> 22 us
  blocking collectives: 25.8 us -> 15.2 us
  waiting for transfers between devices: 200 us -> 190 us
    dot_general x24 -> x0, matrix products: 63.5 us -> none  [the longest x8 38.6 us: layer_part(): jnp.dot(normed, weight_in, preferred_element_type=jnp.float32)]
    ppermute x15 -> x16, waiting for transfers between devices: 125 us -> 61.5 us  [the longest x10 52.2 us: body(): arriving = lax.ppermute(previous, 'chip', forward)]
    all_gather x1, waiting for transfers between devices: 57.2 us -> 113 us  [on_device(): mine = lax.all_gather(shard, DP, axis=0, tiled=True)]
    pallas_call x0 -> x11, Pallas kernels: none -> 47.6 us  [the longest x10 46.9 us: stage(): pl.pallas_call(stage_kernel, out_shape=(jax.ShapeDtypeStruct(out.shape, o...]
    dynamic_update_slice x15 -> x0, other arithmetic: 25.9 us -> none  [tick(): lax.dynamic_update_slice(saved, jnp.where(valid, finished[None], previous...]
    ppermute x15 -> x16, starting transfers between devices: 38.9 us -> 18.1 us  [the longest x10 12.9 us: body(): arriving = lax.ppermute(previous, 'chip', forward)]
    cond x40 -> x0, local copies, waits for them, and re-layouts: 20 us -> none
    reshape x16 -> x0, local copies, waits for them, and re-layouts: 16.6 us -> none  [the longest x8 9.89 us: layer_part(): jnp.einsum('hqk,khd->qhd', weights, values, preferred_element_type=jnp.fl...]
  transfers between devices with their start and end apart: 18 -> 18, of which waited for: 16 -> 14; matrix products, arithmetic and copies ran while one was open for 9% -> 3% of each run, Pallas kernels for 0% -> 15%
where the time goes in v1:
time: 312 us; the launch traced here: 311 us
  waiting for transfers between devices  190 us (61%)
  Pallas kernels  47.6 us (15%)
  starting transfers between devices  22 us (7%)
  local copies, waits for them, and re-layouts  15.9 us (5%)
  blocking collectives  15.2 us (5%)
  between operations  13.7 us (4%)
  other arithmetic  6.75 us (2%)
    all_gather x1, waiting for transfers between devices, on_device(): mine = lax.all_gather(shard, DP, axis=0, tiled=True)  113 us
    ppermute x10, waiting for transfers between devices, body(): arriving = lax.ppermute(previous, 'chip', forward)  52.2 us
    pallas_call x10, Pallas kernels, stage(): pl.pallas_call(stage_kernel, out_shape=(jax.ShapeDtypeStruct(out.shape, o...  46.9 us
    all_to_all x1, blocking collectives, lookup_items(): lax.all_to_all(request, DP, split_axis=0, concat_axis=0, tiled=True)  15.2 us
    all_to_all x1, waiting for transfers between devices, lookup_items(): lax.all_to_all(found.reshape(groups, slots_each, -1), DP, split_axis=0, c...  15.2 us
    ppermute x10, starting transfers between devices, body(): arriving = lax.ppermute(previous, 'chip', forward)  12.9 us
    while x10, local copies, waits for them, and re-layouts  9.51 us
  transfers between devices with their start and end apart: 18, of which 14 were waited for; matrix products, arithmetic and copies ran while one was open for 3% of the time, Pallas kernels for 15%

profile of v1, /device:TPU:6, one launch (start us, length us, event | category | flops | bytes accessed | tf_op | source)
XLA Modules:
  0.0 311.0 jit_solution(7903434673544392760)
XLA Ops:
  6.5 1.8 pad_maximum_fusion.1
  8.4 113.0 %all-gather.2.cloned.1.call-done = bf16[1024,5120]{1,0:T(8,128)(2,1)} async-done(((bf16[32,5120]{1,0:T(8,128)(2,1)}), bf16[1024,5120]{1,0:T(8,128)(2,1)}) %all-gather.2.cloned.1.call-update) | async-done | bytes 10485776 | tf_op jit(solution)/shard_map/all_gather | solution.py:267
  121.3 0.7 fusion
  122.1 0.2 reduce_window_sum.11
  122.3 0.8 select_reduce_fusion
  123.1 1.3 multiply_reduce_fusion
  124.4 15.2 %all_to_all.14 = s32[32,1,8]{2,1,0:T(1,128)S(1)} all-to-all(s32[32,1,8]{2,1,0:T(1,128)S(1)} %bitcast.35), channel_id=1, replica_groups=mesh['chip'=4,'core'=2,'dp_0'=4,'dp_1'=8] {'dp_0','dp_1'}, dimensions={0} | all-to-all | bytes 2048 | tf_op jit(solution)/shard_map/all_to_all | solution.py:250
  139.7 0.5 broadcast.55
  140.2 0.7 reduce.3
  141.0 2.0 gather_fusion
  143.0 3.9 %all-to-all-start.1 = ((bf16[32,8,1024]{2,1,0:T(8,128)(2,1)}), bf16[32,8,1024]{2,1,0:T(8,128)(2,1)S(1)}, u32[]{:S(2)}, u32[]{:S(2)}) async-start(bf16[32,8,1024]{2,1,0:T(8,128)(2,1)} %bitcast.8), calls=%async_computation.1 | async-start | bytes 1048576 | tf_op jit(solution)/shard_map/all_to_all | solution.py:252
  147.2 1.0 collective-permute-done.5
  148.2 15.2 %all-to-all-done.1 = bf16[32,8,1024]{2,1,0:T(8,128)(2,1)S(1)} async-done(((bf16[32,8,1024]{2,1,0:T(8,128)(2,1)}), bf16[32,8,1024]{2,1,0:T(8,128)(2,1)S(1)}, u32[]{:S(2)}, u32[]{:S(2)}) %all-to-all-start.1) | async-done | bytes 524320 | tf_op jit(solution)/shard_map/all_to_all | solution.py:252
  163.4 0.9 gather_fusion.1
  164.3 0.7 collective-permute-start.2
  165.0 0.7 collective-permute-start.1
  165.7 3.7 %collective-permute-start.3 = (bf16[128,1024]{1,0:T(8,128)(2,1)S(1)}, bf16[128,1024]{1,0:T(8,128)(2,1)S(1)}, u32[]{:S(2)}, u32[]{:S(2)}) collective-permute-start(bf16[128,1024]{1,0:T(8,128)(2,1)S(1)} %gather_fusion.1), channel_id=1, source_target_pairs={{192,0},{193,1},{194,2},{195,3},{196,4},{197,5},{198,6},{199,7},{2... | collective-permute-start | bytes 786440 | tf_op jit(solution)/shard_map/ppermute | solution.py:270
  169.4 5.4 %collective-permute-done.3 = bf16[128,1024]{1,0:T(8,128)(2,1)S(1)} collective-permute-done((bf16[128,1024]{1,0:T(8,128)(2,1)S(1)}, bf16[128,1024]{1,0:T(8,128)(2,1)S(1)}, u32[]{:S(2)}, u32[]{:S(2)}) %collective-permute-start.3) | collective-permute-done | bytes 262176 | tf_op jit(solution)/shard_map/ppermute | solution.py:270
  174.9 1.1 pad_maximum_fusion
  176.0 1.1 broadcast_in_dim.23
  177.1 0.3 broadcast_in_dim.22
  177.4 121.9 %while.19 = (s32[]{:T(128)}, bf16[8,128,1024]{2,1,0:T(8,128)(2,1)S(1)}, bf16[4,128,1024]{2,1,0:T(8,128)(2,1)}, bf16[128,1024]{1,0:T(8,128)(2,1)S(1)}, bf16[128,1...) while((s32[]{:T(128)}, ...), condition=%wide.region_4.5_spmd, body=%wide.region_3.4_spmd.sunk | while | flops 2684354560 | bytes 23068836 | solution.py:296
  177.4 1.3 collective-permute-start
  178.7 0.9 eval_jaxpr.5
  179.7 6.3 %collective-permute-done = bf16[128,1024]{1,0:T(8,128)(2,1)} collective-permute-done((bf16[128,1024]{1,0:T(8,128)(2,1)S(1)}, bf16[128,1024]{1,0:T(8,128)(2,1)}, u32[]{:S(2)}, u32[]{:S(2)}) %collective-permute-start) | collective-permute-done | bytes 262176 | tf_op jit(solution)/shard_map/while/body/eval_jaxpr/ppermute | solution.py:290
  186.0 1.0 copy.30
  187.0 1.3 collective-permute-start
  188.3 0.9 eval_jaxpr.5
  189.2 6.1 %collective-permute-done = bf16[128,1024]{1,0:T(8,128)(2,1)} collective-permute-done((bf16[128,1024]{1,0:T(8,128)(2,1)S(1)}, bf16[128,1024]{1,0:T(8,128)(2,1)}, u32[]{:S(2)}, u32[]{:S(2)}) %collective-permute-start) | collective-permute-done | bytes 262176 | tf_op jit(solution)/shard_map/while/body/eval_jaxpr/ppermute | solution.py:290
  195.4 1.0 copy.30
  196.3 1.3 collective-permute-start
  197.6 0.9 eval_jaxpr.5
  198.6 6.1 %collective-permute-done = bf16[128,1024]{1,0:T(8,128)(2,1)} collective-permute-done((bf16[128,1024]{1,0:T(8,128)(2,1)S(1)}, bf16[128,1024]{1,0:T(8,128)(2,1)}, u32[]{:S(2)}, u32[]{:S(2)}) %collective-permute-start) | collective-permute-done | bytes 262176 | tf_op jit(solution)/shard_map/while/body/eval_jaxpr/ppermute | solution.py:290
  204.7 1.0 copy.30
  205.7 1.3 collective-permute-start
  207.0 0.9 eval_jaxpr.5
  207.9 8.4 %collective-permute-done = bf16[128,1024]{1,0:T(8,128)(2,1)} collective-permute-done((bf16[128,1024]{1,0:T(8,128)(2,1)S(1)}, bf16[128,1024]{1,0:T(8,128)(2,1)}, u32[]{:S(2)}, u32[]{:S(2)}) %collective-permute-start) | collective-permute-done | bytes 262176 | tf_op jit(solution)/shard_map/while/body/eval_jaxpr/ppermute | solution.py:290
  216.3 1.0 copy.30
  217.3 1.3 collective-permute-start
  218.6 0.9 eval_jaxpr.5
  219.5 10.2 %collective-permute-done = bf16[128,1024]{1,0:T(8,128)(2,1)} collective-permute-done((bf16[128,1024]{1,0:T(8,128)(2,1)S(1)}, bf16[128,1024]{1,0:T(8,128)(2,1)}, u32[]{:S(2)}, u32[]{:S(2)}) %collective-permute-start) | collective-permute-done | bytes 262176 | tf_op jit(solution)/shard_map/while/body/eval_jaxpr/ppermute | solution.py:290
  229.7 1.0 copy.30
  230.7 1.3 collective-permute-start
  232.0 0.9 eval_jaxpr.5
  232.9 10.2 %collective-permute-done = bf16[128,1024]{1,0:T(8,128)(2,1)} collective-permute-done((bf16[128,1024]{1,0:T(8,128)(2,1)S(1)}, bf16[128,1024]{1,0:T(8,128)(2,1)}, u32[]{:S(2)}, u32[]{:S(2)}) %collective-permute-start) | collective-permute-done | bytes 262176 | tf_op jit(solution)/shard_map/while/body/eval_jaxpr/ppermute | solution.py:290
  243.1 1.0 copy.30
  244.0 1.3 collective-permute-start
  245.3 10.3 %eval_jaxpr.5 = (bf16[8,128,1024]{2,1,0:T(8,128)(2,1)S(1)}, bf16[4,128,1024]{2,1,0:T(8,128)(2,1)}, bf16[128,1024]{1,0:T(8,128)(2,1)S(1)}) custom-call(s32[1]{0:T(128)} %bitcast.27.step_ref, s32[16]{0:T(128)S(1)} %get-tuple-element.312.info_ref, bf16[4,128,1024]{2,1,0:T(8,128)(2,1)} %get-tuple-element.313.inputs_ref, ...), custom_call_target="tpu_custom_call", output_to_operand_aliasing={{0}: (8, {}), {1}: (9, {})} | custom-call | flops 2684354560 | bytes 20971520 | tf_op jit(solution)/shard_map/while/body/eval_jaxpr/pallas_call | solution.py:181
  255.7 0.8 collective-permute-done
  256.4 1.0 copy.30
  257.4 1.3 collective-permute-start
  258.7 10.3 %eval_jaxpr.5 = (bf16[8,128,1024]{2,1,0:T(8,128)(2,1)S(1)}, bf16[4,128,1024]{2,1,0:T(8,128)(2,1)}, bf16[128,1024]{1,0:T(8,128)(2,1)S(1)}) custom-call(s32[1]{0:T(128)} %bitcast.27.step_ref, s32[16]{0:T(128)S(1)} %get-tuple-element.312.info_ref, bf16[4,128,1024]{2,1,0:T(8,128)(2,1)} %get-tuple-element.313.inputs_ref, ...), custom_call_target="tpu_custom_call", output_to_operand_aliasing={{0}: (8, {}), {1}: (9, {})} | custom-call | flops 2684354560 | bytes 20971520 | tf_op jit(solution)/shard_map/while/body/eval_jaxpr/pallas_call | solution.py:181
  269.0 1.9 collective-permute-done
  271.0 1.0 copy.30
  271.9 1.3 collective-permute-start
  273.2 10.3 %eval_jaxpr.5 = (bf16[8,128,1024]{2,1,0:T(8,128)(2,1)S(1)}, bf16[4,128,1024]{2,1,0:T(8,128)(2,1)}, bf16[128,1024]{1,0:T(8,128)(2,1)S(1)}) custom-call(s32[1]{0:T(128)} %bitcast.27.step_ref, s32[16]{0:T(128)S(1)} %get-tuple-element.312.info_ref, bf16[4,128,1024]{2,1,0:T(8,128)(2,1)} %get-tuple-element.313.inputs_ref, ...), custom_call_target="tpu_custom_call", output_to_operand_aliasing={{0}: (8, {}), {1}: (9, {})} | custom-call | flops 2684354560 | bytes 20971520 | tf_op jit(solution)/shard_map/while/body/eval_jaxpr/pallas_call | solution.py:181
  283.5 2.2 collective-permute-done
  285.7 1.0 copy.30
  286.7 1.3 collective-permute-start
  288.0 10.3 %eval_jaxpr.5 = (bf16[8,128,1024]{2,1,0:T(8,128)(2,1)S(1)}, bf16[4,128,1024]{2,1,0:T(8,128)(2,1)}, bf16[128,1024]{1,0:T(8,128)(2,1)S(1)}) custom-call(s32[1]{0:T(128)} %bitcast.27.step_ref, s32[16]{0:T(128)S(1)} %get-tuple-element.312.info_ref, bf16[4,128,1024]{2,1,0:T(8,128)(2,1)} %get-tuple-element.313.inputs_ref, ...), custom_call_target="tpu_custom_call", output_to_operand_aliasing={{0}: (8, {}), {1}: (9, {})} | custom-call | flops 2684354560 | bytes 20971520 | tf_op jit(solution)/shard_map/while/body/eval_jaxpr/pallas_call | solution.py:181
  298.3 1.0 copy.30
  299.3 2.9 collective-permute-done.6.received
  302.2 0.7 shard_map.82
  302.9 1.3 copy-done.1
  (45 shorter events, 0.7 us)
Async XLA Ops:
  6.5 134.4 %copy-start = (bf16[256,1024]{1,0:T(8,128)(2,1)S(1)}, bf16[256,1024]{1,0:T(8,128)(2,1)}, u32[]{:S(2)}) copy-start(bf16[256,1024]{1,0:T(8,128)(2,1)} %param.13) | copy-start | bytes 1572868
  6.5 114.8 %all-gather.2.cloned.1.call-start = ((), (), s32[]{:S(2)}) async-start(), calls=%async_computation.2 | async-start | bytes 10813440 | tf_op jit(solution)/shard_map/all_gather | solution.py:267
  121.3 54.7 %collective-permute-start.4 = (bf16[1024,5120]{1,0:T(8,128)(2,1)}, bf16[1024,5120]{1,0:T(8,128)(2,1)}, u32[]{:S(2)}, u32[]{:S(2)}) collective-permute-start(bf16[1024,5120]{1,0:T(8,128)(2,1)} %all-gather.2.cloned.1.call-done), channel_id=1, source_target_pairs={{0,32},{32,0},{1,33},{33,1},{2,34},{34,2},{3,35},{35,3},{4,36},{36... | collective-permute-start | bytes 31457288 | tf_op jit(solution)/shard_map/ppermute | solution.py:260
  141.0 5.9 %copy-start.2 = (f32[1,1024]{1,0:T(1,128)S(1)}, f32[1,1024]{1,0:T(1,128)}, u32[]{:S(2)}) copy-start(f32[1,1024]{1,0:T(1,128)} %param.17) | copy-start | bytes 12292
  141.0 5.9 %copy-start.3 = (f32[1,1024]{1,0:T(1,128)S(1)}, f32[1,1024]{1,0:T(1,128)}, u32[]{:S(2)}) copy-start(f32[1,1024]{1,0:T(1,128)} %param.16) | copy-start | bytes 12292
  141.0 6.0 %copy-start.4 = (s32[1,1,128,1]{2,3,1,0:T(1,128)S(1)}, s32[1,1,128,1]{2,3,1,0:T(1,128)}, u32[]{:S(2)}) copy-start(s32[1,1,128,1]{2,3,1,0:T(1,128)} %param.10) | copy-start | bytes 1540
  141.0 6.1 %copy-start.5 = (s32[8,1]{0,1:T(1,128)S(1)}, s32[8,1]{0,1:T(1,128)}, u32[]{:S(2)}) copy-start(s32[8,1]{0,1:T(1,128)} %param.12) | copy-start | bytes 100
  143.0 20.4 %all-to-all-start.1 = ((bf16[32,8,1024]{2,1,0:T(8,128)(2,1)}), bf16[32,8,1024]{2,1,0:T(8,128)(2,1)S(1)}, u32[]{:S(2)}, u32[]{:S(2)}) async-start(bf16[32,8,1024]{2,1,0:T(8,128)(2,1)} %bitcast.8), calls=%async_computation.1 | async-start | bytes 1048576 | tf_op jit(solution)/shard_map/all_to_all | solution.py:252
  146.9 1.3 collective-permute-start.5
  164.3 5.1 %collective-permute-start.2 = (bf16[128,1024]{1,0:T(8,128)(2,1)S(1)}, bf16[128,1024]{1,0:T(8,128)(2,1)S(1)}, u32[]{:S(2)}, u32[]{:S(2)}) collective-permute-start(bf16[128,1024]{1,0:T(8,128)(2,1)S(1)} %gather_fusion.1), channel_id=1, source_target_pairs={{128,0},{129,1},{130,2},{131,3},{132,4},{133,5},{134,6},{135,7},{1... | collective-permute-start | bytes 786440 | tf_op jit(solution)/shard_map/ppermute | solution.py:270
  165.0 4.5 %collective-permute-start.1 = (bf16[128,1024]{1,0:T(8,128)(2,1)S(1)}, bf16[128,1024]{1,0:T(8,128)(2,1)S(1)}, u32[]{:S(2)}, u32[]{:S(2)}) collective-permute-start(bf16[128,1024]{1,0:T(8,128)(2,1)S(1)} %gather_fusion.1), channel_id=1, source_target_pairs={{64,0},{65,1},{66,2},{67,3},{68,4},{69,5},{70,6},{71,7},{72,8},{73... | collective-permute-start | bytes 786440 | tf_op jit(solution)/shard_map/ppermute | solution.py:270
  165.7 9.2 %collective-permute-start.3 = (bf16[128,1024]{1,0:T(8,128)(2,1)S(1)}, bf16[128,1024]{1,0:T(8,128)(2,1)S(1)}, u32[]{:S(2)}, u32[]{:S(2)}) collective-permute-start(bf16[128,1024]{1,0:T(8,128)(2,1)S(1)} %gather_fusion.1), channel_id=1, source_target_pairs={{192,0},{193,1},{194,2},{195,3},{196,4},{197,5},{198,6},{199,7},{2... | collective-permute-start | bytes 786440 | tf_op jit(solution)/shard_map/ppermute | solution.py:270
  177.4 8.6 %collective-permute-start = (bf16[128,1024]{1,0:T(8,128)(2,1)S(1)}, bf16[128,1024]{1,0:T(8,128)(2,1)}, u32[]{:S(2)}, u32[]{:S(2)}) collective-permute-start(bf16[128,1024]{1,0:T(8,128)(2,1)S(1)} %copy.24), channel_id=1, source_target_pairs={{0,64},{64,128},{128,192},{1,65},{65,129},{129,193},{2,66},{66,130... | collective-permute-start | bytes 786440 | tf_op jit(solution)/shard_map/while/body/eval_jaxpr/ppermute | solution.py:290
  187.0 8.4 %collective-permute-start = (bf16[128,1024]{1,0:T(8,128)(2,1)S(1)}, bf16[128,1024]{1,0:T(8,128)(2,1)}, u32[]{:S(2)}, u32[]{:S(2)}) collective-permute-start(bf16[128,1024]{1,0:T(8,128)(2,1)S(1)} %copy.24), channel_id=1, source_target_pairs={{0,64},{64,128},{128,192},{1,65},{65,129},{129,193},{2,66},{66,130... | collective-permute-start | bytes 786440 | tf_op jit(solution)/shard_map/while/body/eval_jaxpr/ppermute | solution.py:290
  196.3 8.4 %collective-permute-start = (bf16[128,1024]{1,0:T(8,128)(2,1)S(1)}, bf16[128,1024]{1,0:T(8,128)(2,1)}, u32[]{:S(2)}, u32[]{:S(2)}) collective-permute-start(bf16[128,1024]{1,0:T(8,128)(2,1)S(1)} %copy.24), channel_id=1, source_target_pairs={{0,64},{64,128},{128,192},{1,65},{65,129},{129,193},{2,66},{66,130... | collective-permute-start | bytes 786440 | tf_op jit(solution)/shard_map/while/body/eval_jaxpr/ppermute | solution.py:290
  205.7 10.6 %collective-permute-start = (bf16[128,1024]{1,0:T(8,128)(2,1)S(1)}, bf16[128,1024]{1,0:T(8,128)(2,1)}, u32[]{:S(2)}, u32[]{:S(2)}) collective-permute-start(bf16[128,1024]{1,0:T(8,128)(2,1)S(1)} %copy.24), channel_id=1, source_target_pairs={{0,64},{64,128},{128,192},{1,65},{65,129},{129,193},{2,66},{66,130... | collective-permute-start | bytes 786440 | tf_op jit(solution)/shard_map/while/body/eval_jaxpr/ppermute | solution.py:290
  217.3 12.4 %collective-permute-start = (bf16[128,1024]{1,0:T(8,128)(2,1)S(1)}, bf16[128,1024]{1,0:T(8,128)(2,1)}, u32[]{:S(2)}, u32[]{:S(2)}) collective-permute-start(bf16[128,1024]{1,0:T(8,128)(2,1)S(1)} %copy.24), channel_id=1, source_target_pairs={{0,64},{64,128},{128,192},{1,65},{65,129},{129,193},{2,66},{66,130... | collective-permute-start | bytes 786440 | tf_op jit(solution)/shard_map/while/body/eval_jaxpr/ppermute | solution.py:290
  230.7 12.4 %collective-permute-start = (bf16[128,1024]{1,0:T(8,128)(2,1)S(1)}, bf16[128,1024]{1,0:T(8,128)(2,1)}, u32[]{:S(2)}, u32[]{:S(2)}) collective-permute-start(bf16[128,1024]{1,0:T(8,128)(2,1)S(1)} %copy.24), channel_id=1, source_target_pairs={{0,64},{64,128},{128,192},{1,65},{65,129},{129,193},{2,66},{66,130... | collective-permute-start | bytes 786440 | tf_op jit(solution)/shard_map/while/body/eval_jaxpr/ppermute | solution.py:290
  244.0 12.4 %collective-permute-start = (bf16[128,1024]{1,0:T(8,128)(2,1)S(1)}, bf16[128,1024]{1,0:T(8,128)(2,1)}, u32[]{:S(2)}, u32[]{:S(2)}) collective-permute-start(bf16[128,1024]{1,0:T(8,128)(2,1)S(1)} %copy.24), channel_id=1, source_target_pairs={{0,64},{64,128},{128,192},{1,65},{65,129},{129,193},{2,66},{66,130... | collective-permute-start | bytes 786440 | tf_op jit(solution)/shard_map/while/body/eval_jaxpr/ppermute | solution.py:290
  257.4 13.5 %collective-permute-start = (bf16[128,1024]{1,0:T(8,128)(2,1)S(1)}, bf16[128,1024]{1,0:T(8,128)(2,1)}, u32[]{:S(2)}, u32[]{:S(2)}) collective-permute-start(bf16[128,1024]{1,0:T(8,128)(2,1)S(1)} %copy.24), channel_id=1, source_target_pairs={{0,64},{64,128},{128,192},{1,65},{65,129},{129,193},{2,66},{66,130... | collective-permute-start | bytes 786440 | tf_op jit(solution)/shard_map/while/body/eval_jaxpr/ppermute | solution.py:290
  271.9 13.8 %collective-permute-start = (bf16[128,1024]{1,0:T(8,128)(2,1)S(1)}, bf16[128,1024]{1,0:T(8,128)(2,1)}, u32[]{:S(2)}, u32[]{:S(2)}) collective-permute-start(bf16[128,1024]{1,0:T(8,128)(2,1)S(1)} %copy.24), channel_id=1, source_target_pairs={{0,64},{64,128},{128,192},{1,65},{65,129},{129,193},{2,66},{66,130... | collective-permute-start | bytes 786440 | tf_op jit(solution)/shard_map/while/body/eval_jaxpr/ppermute | solution.py:290
  286.7 11.6 %collective-permute-start = (bf16[128,1024]{1,0:T(8,128)(2,1)S(1)}, bf16[128,1024]{1,0:T(8,128)(2,1)}, u32[]{:S(2)}, u32[]{:S(2)}) collective-permute-start(bf16[128,1024]{1,0:T(8,128)(2,1)S(1)} %copy.24), channel_id=1, source_target_pairs={{0,64},{64,128},{128,192},{1,65},{65,129},{129,193},{2,66},{66,130... | collective-permute-start | bytes 786440 | tf_op jit(solution)/shard_map/while/body/eval_jaxpr/ppermute | solution.py:290
  299.3 2.9 collective-permute-start.6
  302.8 1.3 copy-start.1
Sparse Core Ops, SparseCore 0:
  9.9 111.3 all-gather.1
